TPU v7x, 32 devices: a whole 2x2x4 slice. The times are simulated.
32 devices in a mesh: grp: 4 (over y, x), tp: 8 (over z, core).
Axes of the slice: x: 2, y: 2, z: 4, core: 2. Of those that a mesh axis runs over, the one named last changes fastest.
Arguments:
- tokens: bfloat16 [1280, 4096], P(('grp', 'tp')), may hold values from -6 to 6
- norm_gain: float32 [4096], replicated, may hold values from 0.5 to 1.5
- spill_blocks: int32 [1], replicated, may hold values from 0 to 7, as said below
- image_gate: bfloat16 [4096, 11008], P('grp', 'tp'), may hold values from -0.09375 to 0.09375
- image_up: bfloat16 [4096, 11008], P('grp', 'tp'), may hold values from -0.09375 to 0.09375
- image_down: bfloat16 [11008, 4096], P('tp', 'grp'), may hold values from -0.0546875 to 0.0546875
- text_gate: bfloat16 [4096, 11008], P(None, 'tp'), may hold values from -0.09375 to 0.09375
- text_up: bfloat16 [4096, 11008], P(None, 'tp'), may hold values from -0.09375 to 0.09375
- text_down: bfloat16 [11008, 4096], P('tp'), may hold values from -0.0546875 to 0.0546875
Outputs:
- mixed: bfloat16 [1280, 4096], P(('grp', 'tp'))
Inputs may be any that keep to these rules, and one draw needn't show every extreme that they name: `spill_blocks`: 1 distinct indices of 0 to 8 - 1, in increasing order.
All inputs are finite; a program needn't handle non-finite values.
Results may differ from a plain program's by a relative error of at most 0.0046.
Values may be sent and summed in bfloat16 or wider, within the bound.
A program may use at most 256 MiB of HBM per device.

v0:
```python
import jax
import jax.numpy as jnp
from jax import lax
from jax.sharding import PartitionSpec as P

norm_epsilon = 1e-05


def hidden_of(inputs, w_gate, w_up):
    gate_out = jnp.dot(inputs, w_gate, preferred_element_type=jnp.float32)
    up_out = jnp.dot(inputs, w_up, preferred_element_type=jnp.float32)
    return (jax.nn.silu(gate_out) * up_out).astype(jnp.bfloat16)


def feed_forward(inputs, w_gate, w_up, w_down):
    hidden = hidden_of(inputs, w_gate, w_up)
    return jnp.dot(hidden, w_down, preferred_element_type=jnp.float32)


def on_device(
    tokens, norm_gain, spill_blocks, image_gate, image_up, image_down, text_gate, text_up, text_down
):
    block_rows = tokens.shape[0]
    model_width = tokens.shape[1]
    shard_count = lax.axis_size("tp")
    group_count = lax.axis_size("grp")
    group_id = lax.axis_index("grp")
    spill_count = spill_blocks.shape[0]
    in_text = group_id == group_count - 1
    tokens_wide = tokens.astype(jnp.float32)
    scale = lax.rsqrt(jnp.mean(tokens_wide * tokens_wide, axis=-1, keepdims=True) + norm_epsilon)
    normed = (tokens_wide * scale * norm_gain).astype(jnp.bfloat16)
    image_gate_all, image_up_all, image_down_all = (
        lax.all_gather(image_gate, "grp", axis=0, tiled=True),
        lax.all_gather(image_up, "grp", axis=0, tiled=True),
        lax.all_gather(image_down, "grp", axis=1, tiled=True),
    )
    spill_mask = jnp.any(
        jnp.arange(shard_count, dtype=jnp.int32)[:, None] == spill_blocks[None, :], axis=1
    )
    hidden_units = text_gate.shape[1]
    gate_pick = jnp.where(in_text, text_gate, image_gate_all)
    up_pick = jnp.where(in_text, text_up, image_up_all)
    piece = lax.all_gather(normed, "tp", axis=0, tiled=True)
    joined = jnp.concatenate([hidden_of(piece, gate_pick, up_pick), piece], axis=1)
    hidden_all = joined[:, :hidden_units]
    grouped = joined[:, hidden_units:]
    blocks = grouped.reshape(shard_count, block_rows, model_width)
    spill_input = blocks[spill_blocks].reshape(-1, model_width)
    empty_terms = jnp.zeros((spill_count * block_rows, model_width), jnp.float32)

    def spill_compute():
        return feed_forward(spill_input, image_gate_all, image_up_all, image_down_all)

    spill_out = lax.cond(in_text, spill_compute, lambda: empty_terms)
    placed = jnp.zeros((shard_count, block_rows, model_width), jnp.float32)
    placed = placed.at[spill_blocks].set(spill_out.reshape(spill_count, block_rows, model_width))
    placed = jnp.where(in_text, placed.reshape(-1, model_width), 0.0)
    row_spill = jnp.broadcast_to(spill_mask[:, None], (shard_count, block_rows)).reshape(-1)
    row_spill = jnp.logical_and(row_spill, in_text)
    hidden_kept = jnp.where(row_spill[:, None], jnp.zeros((), jnp.bfloat16), hidden_all)
    down_pick = jnp.where(in_text, text_down, image_down_all)
    summed = lax.psum_scatter(
        jnp.dot(hidden_kept, down_pick, preferred_element_type=jnp.float32) + placed,
        "tp",
        scatter_dimension=0,
        tiled=True,
    )
    return (tokens_wide + summed).astype(jnp.bfloat16)


def solution(mesh):
    in_specs = (
        P(("grp", "tp"), None),
        P(),
        P(),
        P("grp", "tp"),
        P("grp", "tp"),
        P("tp", "grp"),
        P(None, "tp"),
        P(None, "tp"),
        P("tp", None),
    )
    out_specs = P(("grp", "tp"), None)
    return jax.shard_map(
        on_device, mesh=mesh, in_specs=in_specs, out_specs=out_specs, check_vma=False
    )
```

profile of v0, /device:TPU:0, one launch (start us, length us, event | category | flops | bytes accessed | tf_op | source)
XLA Modules:
  0.0 512.0 jit_solution(8226217250411875243)
XLA Ops:
  6.5 0.0 copy-start.1
  6.5 0.0 all-gather.5.cloned.1.call-start
  6.5 1.3 fusion.40
  7.8 1.9 fusion.42
  9.7 0.0 all-gather.5.cloned.1.call-update
  9.7 0.0 all-gather.11.cloned.1.call-start
  9.8 0.7 all-gather.11.cloned.1.call-update
  10.5 0.0 all-gather.7.cloned.1.call-start
  10.5 0.0 copy-done.1
  10.5 2.9 copy.10
  13.5 0.0 all-gather.7.cloned.1.call-update
  13.5 0.0 all-gather.9.cloned.1.call-start
  13.5 4.6 copy.12
  18.1 0.0 all-gather.9.cloned.1.call-update
  18.1 0.0 reduce-scatter.2.cloned.1.call-start
  18.8 0.1 broadcast_in_dim.36
  18.9 0.1 and.23
  19.0 15.3 %copy.11 = bf16[4096,1376]{1,0:T(8,128)(2,1)} copy(bf16[4096,1376]{0,1:T(8,128)(2,1)} %param.19) | data formatting | bytes 22544384 | tf_op args[6]
  34.3 0.0 copy-start.3
  34.3 15.1 %copy.13 = bf16[4096,1376]{1,0:T(8,128)(2,1)} copy(bf16[4096,1376]{0,1:T(8,128)(2,1)} %param.20) | data formatting | bytes 22544384 | tf_op args[7]
  49.4 0.0 copy-done.3
  49.4 0.7 and_reduce_fusion
  50.1 0.0 all-gather.5.cloned.1.call-done
  50.1 108.7 %all-gather.11.cloned.1.call-done = bf16[1376,4096]{1,0:T(8,128)(2,1)} async-done(((bf16[1376,1024]{1,0:T(8,128)(2,1)}), bf16[1376,4096]{1,0:T(8,128)(2,1)}) %all-gather.11.cloned.1.call-update) | async-done | bytes 11272208 | tf_op jit(solution)/shard_map/all_gather | solution.py:36
  158.8 115.5 %all-gather.7.cloned.1.call-done = bf16[4096,1376]{1,0:T(8,128)(2,1)} async-done(((bf16[1024,1376]{1,0:T(8,128)(2,1)}), bf16[4096,1376]{1,0:T(8,128)(2,1)}) %all-gather.7.cloned.1.call-update) | async-done | bytes 11272208 | tf_op jit(solution)/shard_map/all_gather | solution.py:34
  274.4 115.4 %all-gather.9.cloned.1.call-done = bf16[4096,1376]{1,0:T(8,128)(2,1)} async-done(((bf16[1024,1376]{1,0:T(8,128)(2,1)}), bf16[4096,1376]{1,0:T(8,128)(2,1)}) %all-gather.9.cloned.1.call-update) | async-done | bytes 11272208 | tf_op jit(solution)/shard_map/all_gather | solution.py:35
  389.7 0.2 conditional.1
  390.0 0.0 copy-start.2
  390.0 2.9 broadcast_in_dim.39
  392.9 0.0 slice-start
  392.9 1.7 bitcast_dynamic-update-slice_fusion
  394.6 0.0 copy-done.2
  394.6 0.0 slice-start.1
  394.6 0.0 slice-start.2
  394.6 8.5 %fusion.21 = f32[320,1376]{1,0:T(8,128)} fusion(bf16[320,4096]{1,0:T(8,128)(2,1)S(1)} %copy-done.2, bf16[4096,1376]{1,0:T(8,128)(2,1)} %copy.11, bf16[4096,1376]{1,0:T(8,128)(2,1)} %all-gather.7.cloned.1.call-done, pred[]{:T(512)S(6)} %eq.22), kind=kOutput, calls=%fused_computation.19 | convolution fusion | flops 3612737536 | bytes 26927104 | tf_op jit(solution)/shard_map/dot_general | solution.py:10
  403.1 0.0 slice-done
  403.1 0.0 slice-done.1
  403.1 0.0 slice-done.2
  403.1 6.9 %fusion.37 = bf16[320,1376]{1,0:T(8,128)(2,1)} fusion(bf16[320,4096]{1,0:T(8,128)(2,1)S(1)} %copy-done.2, bf16[4096,1376]{1,0:T(8,128)(2,1)} %copy.13, bf16[4096,1376]{1,0:T(8,128)(2,1)S(1)} %bitcast.21, pred[]{:T(512)S(6)} %eq.22, f32[320,1376]{1,0:T(8,128)} %fusion.21, pred[320]{0:T(512)(128)(4,1)S(1)} %and.23), kind=kOutput, calls=%fused_computation.29 | convolution fusion | flops 3615819776 | bytes 27808064 | tf_op jit(solution)/shard_map/dot_general | solution.py:11
  410.0 0.0 copy-start
  410.0 12.6 %fusion.28 = f32[320,4096]{1,0:T(8,128)} fusion(f32[320,4096]{1,0:T(8,128)} %bitcast.6, bf16[320,1376]{1,0:T(8,128)(2,1)} %fusion.37, bf16[1376,4096]{1,0:T(8,128)(2,1)} %param.21, bf16[1376,4096]{1,0:T(8,128)(2,1)} %all-gather.11.cloned.1.call-done, pred[]{:T(512)S(6)} %eq.22), kind=kOutput, calls=%fused_computation.26 | convolution fusion | flops 3614048256 | bytes 33910784 | tf_op jit(solution)/shard_map/dot_general | solution.py:64
  422.6 0.0 reduce-scatter.2.cloned.1.call-update
  422.6 80.9 %reduce-scatter.2.cloned.1.call-done = f32[40,4096]{1,0:T(8,128)} async-done(((f32[320,4096]{1,0:T(8,128)}), f32[40,4096]{1,0:T(8,128)}) %reduce-scatter.2.cloned.1.call-update) | async-done | bytes 655376 | tf_op jit(solution)/shard_map/reduce_scatter | solution.py:63
  503.6 0.0 copy-done
  503.6 1.9 fusion.43
  (4 shorter events, 0.1 us)
Async XLA Ops:
  6.5 4.0 copy-start.1
  6.5 43.6 %all-gather.5.cloned.1.call-start = ((), (), s32[]{:S(2)}) async-start(), calls=%async_computation.1 | async-start | bytes 2949120 | tf_op jit(solution)/shard_map/all_gather | solution.py:44
  9.7 149.1 %all-gather.11.cloned.1.call-start = ((), (), s32[]{:S(2)}) async-start(), calls=%async_computation.4 | async-start | bytes 14090240 | tf_op jit(solution)/shard_map/all_gather | solution.py:36
  10.5 263.9 %all-gather.7.cloned.1.call-start = ((), (), s32[]{:S(2)}) async-start(), calls=%async_computation.2 | async-start | bytes 14417920 | tf_op jit(solution)/shard_map/all_gather | solution.py:34
  13.5 376.3 %all-gather.9.cloned.1.call-start = ((), (), s32[]{:S(2)}) async-start(), calls=%async_computation.3 | async-start | bytes 14417920 | tf_op jit(solution)/shard_map/all_gather | solution.py:35
  18.1 485.5 %reduce-scatter.2.cloned.1.call-start = ((), (), s32[]{:S(2)}) async-start(), calls=%async_computation.5 | async-start | bytes 5898240 | tf_op jit(solution)/shard_map/reduce_scatter | solution.py:63
  34.3 15.1 %copy-start.3 = (s32[3]{0:T(128)S(1)}, s32[3]{0:T(128)}, u32[]{:S(2)}) copy-start(s32[3]{0:T(128)} %constant.50.clone.1) | copy-start | bytes 40
  390.0 4.6 copy-start.2
  392.9 10.2 %slice-start = ((s8[11534336]{0:T(1024)(128)(4,1)}), s8[4194304]{0:T(1024)(128)(4,1)S(1)}, s32[]{:S(2)}) async-start(s8[11534336]{0:T(1024)(128)(4,1)} %bitcast.20), calls=%async_computation.6 | async-start | bytes 8388608
  394.6 8.5 %slice-start.1 = ((s8[11534336]{0:T(1024)(128)(4,1)}), s8[4194304]{0:T(1024)(128)(4,1)S(1)}, s32[]{:S(2)}) async-start(s8[11534336]{0:T(1024)(128)(4,1)} %bitcast.20), calls=%async_computation.7 | async-start | bytes 8388608
  394.6 8.5 %slice-start.2 = ((s8[11534336]{0:T(1024)(128)(4,1)}), s8[3145728]{0:T(1024)(128)(4,1)S(1)}, s32[]{:S(2)}) async-start(s8[11534336]{0:T(1024)(128)(4,1)} %bitcast.20), calls=%async_computation.8 | async-start | bytes 6291456
  410.0 93.6 %copy-start = (bf16[40,4096]{1,0:T(8,128)(2,1)S(1)}, bf16[40,4096]{1,0:T(8,128)(2,1)}, u32[]{:S(2)}) copy-start(bf16[40,4096]{1,0:T(8,128)(2,1)} %param.13) | copy-start | bytes 983044
Sparse Core Ops, SparseCore 0:
  9.8 36.4 all-gather.4
  48.1 110.6 all-gather.10
  160.7 113.6 all-gather.6
  276.1 113.6 all-gather.8
  422.8 80.7 reduce-scatter.1
where the time goes:
time: 513 us; the launch traced here: 512 us
  waiting for transfers between devices  421 us (82%)
  local copies, waits for them, and re-layouts  41 us (8%)
  matrix products  28 us (5%)
  between operations  13.9 us (3%)
  other arithmetic  7.4 us (1%)
    all_gather x1, waiting for transfers between devices, on_device(): lax.all_gather(image_gate, 'grp', axis=0, tiled=True)  116 us
    all_gather x1, waiting for transfers between devices, on_device(): lax.all_gather(image_up, 'grp', axis=0, tiled=True)  115 us
    all_gather x1, waiting for transfers between devices, on_device(): lax.all_gather(image_down, 'grp', axis=1, tiled=True)  109 us
    reduce_scatter x1, waiting for transfers between devices, on_device(): lax.psum_scatter(jnp.dot(hidden_kept, down_pick, preferred_element_type=j...  80.9 us
    unnamed x18, local copies, waits for them, and re-layouts  37.9 us
    dot_general x1, matrix products, on_device(): jnp.dot(hidden_kept, down_pick, preferred_element_type=jnp.float32) + placed  12.6 us
  transfers between devices with their start and end apart: 5, of which 4 were waited for; matrix products, arithmetic and copies ran while one was open for 8% of the time, Pallas kernels for 0%

commit v1 on v0

v1 whole, which is shorter than its diff:
```python
import jax
import jax.numpy as jnp
from jax import lax
from jax.sharding import PartitionSpec as P

norm_epsilon = 1e-05
bf16 = jnp.bfloat16
f32 = jnp.float32


def on_device(
    tokens, norm_gain, spill_blocks, image_gate, image_up, image_down, text_gate, text_up, text_down
):
    rows, width = tokens.shape
    n_tp = lax.axis_size("tp")
    n_grp = lax.axis_size("grp")
    group = lax.axis_index("grp")
    n_spill = spill_blocks.shape[0]
    in_text = group == n_grp - 1
    kslice = image_gate.shape[0]
    units = image_gate.shape[1]
    wide = tokens.astype(f32)
    scale = lax.rsqrt(jnp.mean(wide * wide, axis=-1, keepdims=True) + norm_epsilon)
    normed = (wide * scale * norm_gain).astype(bf16)

    cols = normed.reshape(rows, n_grp, kslice).transpose(1, 0, 2)
    cols = lax.all_to_all(cols, "grp", 0, 0, tiled=True)
    cols = lax.all_gather(cols, "tp", axis=1, tiled=False)
    image_part = cols[: n_grp - 1].reshape(-1, kslice)
    spill_part = cols[n_grp - 1][spill_blocks].reshape(-1, kslice)
    x = jnp.concatenate([image_part, spill_part], axis=0)
    n_rows = x.shape[0]
    step = 16 * n_grp
    padded = (n_rows + step - 1) // step * step
    x = jnp.pad(x, ((0, padded - n_rows), (0, 0)))
    part_gate = jnp.dot(x, image_gate, preferred_element_type=f32).astype(bf16)
    part_up = jnp.dot(x, image_up, preferred_element_type=f32).astype(bf16)
    gate = lax.psum_scatter(part_gate, "grp", scatter_dimension=0, tiled=True)
    up = lax.psum_scatter(part_up, "grp", scatter_dimension=0, tiled=True)

    piece = lax.all_gather(normed, "tp", axis=0, tiled=True)

    def text_ffn():
        g = jnp.dot(piece, text_gate, preferred_element_type=f32)
        u = jnp.dot(piece, text_up, preferred_element_type=f32)
        h = (jax.nn.silu(g) * u).astype(bf16)
        return jnp.dot(h, text_down, preferred_element_type=f32).astype(bf16)

    text_terms = lax.cond(
        in_text, text_ffn, lambda: jnp.zeros((n_tp * rows, width), bf16)
    )
    text_out = lax.psum_scatter(text_terms, "tp", scatter_dimension=0, tiled=True)

    hidden = (jax.nn.silu(gate.astype(f32)) * up.astype(f32)).astype(bf16)
    hidden = lax.all_gather(hidden, "grp", axis=0, tiled=True)
    terms = jnp.dot(hidden, image_down, preferred_element_type=f32).astype(bf16)
    image_terms = terms[: (n_grp - 1) * n_tp * rows].reshape(n_grp - 1, n_tp, rows, kslice)
    spill_terms = terms[(n_grp - 1) * n_tp * rows : n_rows].reshape(n_spill, rows, kslice)
    placed = jnp.zeros((n_tp, rows, kslice), bf16).at[spill_blocks].set(spill_terms)
    every = jnp.concatenate([image_terms, placed[None]], axis=0).transpose(1, 0, 2, 3)
    mine = lax.psum_scatter(every.reshape(n_tp, -1, kslice), "tp", scatter_dimension=0, tiled=True)
    mine = mine.reshape(n_grp, rows, kslice)
    back = lax.all_to_all(mine, "grp", 0, 0, tiled=True)
    branch = back.transpose(1, 0, 2).reshape(rows, width)
    is_spill = jnp.any(lax.axis_index("tp") == spill_blocks)
    use_text = jnp.logical_and(in_text, jnp.logical_not(is_spill))
    branch = jnp.where(use_text, text_out, branch)
    return (wide + branch.astype(f32)).astype(bf16)


def solution(mesh):
    in_specs = (
        P(("grp", "tp"), None),
        P(),
        P(),
        P("grp", "tp"),
        P("grp", "tp"),
        P("tp", "grp"),
        P(None, "tp"),
        P(None, "tp"),
        P("tp", None),
    )
    out_specs = P(("grp", "tp"), None)
    return jax.shard_map(
        on_device, mesh=mesh, in_specs=in_specs, out_specs=out_specs, check_vma=False
    )
```

time: 513 us -> 317 us (0.62)
  waiting for transfers between devices: 421 us -> 248 us
  local copies, waits for them, and re-layouts: 41 us -> 11.2 us
  blocking collectives: 0 us -> 11.6 us
  matrix products: 28 us -> 18 us
    all_gather x3 -> x2, waiting for transfers between devices: 340 us -> 72.5 us  [the longest x1 39.8 us: on_device(): hidden = lax.all_gather(hidden, 'grp', axis=0, tiled=True)]
    reduce_scatter x1 -> x4, waiting for transfers between devices: 80.9 us -> 143 us  [the longest x1 44.3 us: on_device(): up = lax.psum_scatter(part_up, 'grp', scatter_dimension=0, tiled=True)]
    unnamed x18, local copies, waits for them, and re-layouts: 37.9 us -> 3.73 us
    all_gather x1, waiting for transfers between devices: 0.01 us -> 26.3 us  [on_device(): piece = lax.all_gather(normed, 'tp', axis=0, tiled=True)]
    all_to_all x0 -> x1, blocking collectives: none -> 11.6 us  [on_device(): cols = lax.all_to_all(cols, 'grp', 0, 0, tiled=True)]
    dot_general x3, matrix products: 28 us -> 18 us  [the longest x1 6.86 us: on_device(): part_up = jnp.dot(x, image_up, preferred_element_type=f32).astype(bf16)]
    all_to_all x0 -> x1, waiting for transfers between devices: none -> 5.55 us  [on_device(): back = lax.all_to_all(mine, 'grp', 0, 0, tiled=True)]
  transfers between devices with their start and end apart: 5 -> 8, of which waited for: 4 -> 8; matrix products, arithmetic and copies ran while one was open for 8% -> 6% of each run, Pallas kernels for 0% -> 0%
where the time goes in v1:
time: 317 us
  waiting for transfers between devices  248 us (78%)
  matrix products  18 us (6%)
  between operations  14.3 us (5%)
  blocking collectives  11.6 us (4%)
  local copies, waits for them, and re-layouts  11.2 us (4%)
  other arithmetic  10.1 us (3%)
  starting transfers between devices  3.99 us (1%)
    reduce_scatter x1, waiting for transfers between devices, on_device(): up = lax.psum_scatter(part_up, 'grp', scatter_dimension=0, tiled=True)  44.3 us
    all_gather x1, waiting for transfers between devices, on_device(): hidden = lax.all_gather(hidden, 'grp', axis=0, tiled=True)  39.8 us
    reduce_scatter x1, waiting for transfers between devices, on_device(): lax.psum_scatter(every.reshape(n_tp, -1, kslice), 'tp', scatter_dimension...  37.3 us
    all_gather x1, waiting for transfers between devices, on_device(): cols = lax.all_gather(cols, 'tp', axis=1, tiled=False)  32.7 us
    reduce_scatter x1, waiting for transfers between devices, on_device(): gate = lax.psum_scatter(part_gate, 'grp', scatter_dimension=0, tiled=True)  32 us
    reduce_scatter x1, waiting for transfers between devices, on_device(): lax.psum_scatter(text_terms, 'tp', scatter_dimension=0, tiled=True)  29.3 us
    all_gather x1, waiting for transfers between devices, on_device(): piece = lax.all_gather(normed, 'tp', axis=0, tiled=True)  26.3 us
    all_to_all x1, blocking collectives, on_device(): cols = lax.all_to_all(cols, 'grp', 0, 0, tiled=True)  11.6 us
  transfers between devices with their start and end apart: 8, of which 8 were waited for; matrix products, arithmetic and copies ran while one was open for 6% of the time, Pallas kernels for 0%

profile of v1, /device:TPU:0, one launch (start us, length us, event | category | flops | bytes accessed | tf_op | source)
XLA Modules:
  0.0 316.9 jit_solution(15081478361410944292)
XLA Ops:
  6.5 0.0 copy-start
  6.5 0.0 all-gather.9.cloned.1.call-start
  6.5 1.3 fusion.10
  7.8 1.1 fusion.12
  9.0 0.0 copy-start.3
  9.0 0.2 reshape.71
  9.2 0.1 copy.27
  9.3 11.6 %all_to_all.10 = bf16[4,40,1024]{2,1,0:T(8,128)(2,1)S(1)} all-to-all(bf16[4,40,1024]{2,1,0:T(8,128)(2,1)S(1)} %copy.27), channel_id=1, replica_groups=mesh['grp'=4,'tp'=8] {'grp'}, dimensions={0} | all-to-all | bytes 655360 | tf_op jit(solution)/shard_map/all_to_all | solution.py:27
  20.9 1.0 copy.28
  21.9 0.0 all-gather.9.cloned.1.call-update
  21.9 0.0 reduce-scatter.7.cloned.1.call-start
  22.6 32.7 %all-gather.9.cloned.1.call-done = bf16[4,320,1024]{2,0,1:T(4,128)(2,1)} async-done(((bf16[4,40,1024]{2,0,1:T(4,128)(2,1)}), bf16[4,320,1024]{2,0,1:T(4,128)(2,1)}) %all-gather.9.cloned.1.call-update) | async-done | bytes 2621456 | tf_op jit(solution)/shard_map/all_gather | solution.py:28
  55.3 0.0 copy-start.2
  55.3 3.4 %slice.47 = bf16[1,320,1024]{2,0,1:T(2,128)(2,1)S(1)} slice(bf16[4,320,1024]{2,0,1:T(4,128)(2,1)} %all-gather.9.cloned.1.call-done), slice={[3:4], [0:320], [0:1024]} | slice | bytes 1310720 | tf_op jit(solution)/shard_map/slice | solution.py:30
  58.7 0.0 copy-done.3
  58.7 0.2 copy.37
  58.9 0.0 copy-done.2
  58.9 0.7 copy.36
  59.7 0.0 copy-start.5
  59.7 1.3 copy-done.5
  61.0 0.0 copy-done
  61.0 5.0 %convolution_convert_fusion.2 = bf16[1024,1376]{0,1:T(8,128)(2,1)} fusion(bf16[1024,1376]{0,1:T(8,128)(2,1)S(1)} %copy-done, bf16[40,1024]{1,0:T(8,128)(2,1)S(1)} %dynamic-slice_bitcast_fusion, bf16[960,1024]{1,0:T(8,128)(2,1)S(1)} %bitcast.35), kind=kOutput, calls=%fused_computation.8 | convolution fusion | flops 2894430208 | bytes 7684096 | tf_op jit(solution)/shard_map/dot_general | solution.py:36
  66.0 0.0 copy-start.6
  66.0 0.0 reduce-scatter.7.cloned.1.call-update
  66.0 0.0 reduce-scatter.9.cloned.1.call-start
  66.1 1.5 copy-done.6
  67.6 6.9 %convolution_convert_fusion.1 = bf16[1024,1376]{0,1:T(8,128)(2,1)} fusion(bf16[1024,1376]{0,1:T(8,128)(2,1)} %param.17, bf16[40,1024]{1,0:T(8,128)(2,1)S(1)} %dynamic-slice_bitcast_fusion, bf16[960,1024]{1,0:T(8,128)(2,1)S(1)} %bitcast.36), kind=kOutput, calls=%fused_computation.7 | convolution fusion | flops 2894430208 | bytes 7684096 | tf_op jit(solution)/shard_map/dot_general | solution.py:37
  74.4 0.0 copy-start.7
  74.4 0.0 reduce-scatter.9.cloned.1.call-update
  74.4 0.0 all-gather.7.cloned.1.call-start
  74.5 32.0 %reduce-scatter.7.cloned.1.call-done = bf16[256,1376]{0,1:T(8,128)(2,1)} async-done(((bf16[1024,1376]{0,1:T(8,128)(2,1)}), bf16[256,1376]{0,1:T(8,128)(2,1)}) %reduce-scatter.7.cloned.1.call-update) | async-done | bytes 704528 | tf_op jit(solution)/shard_map/reduce_scatter | solution.py:38
  106.5 44.3 %reduce-scatter.9.cloned.1.call-done = bf16[256,1376]{0,1:T(8,128)(2,1)} async-done(((bf16[1024,1376]{0,1:T(8,128)(2,1)}), bf16[256,1376]{0,1:T(8,128)(2,1)}) %reduce-scatter.9.cloned.1.call-update) | async-done | bytes 704528 | tf_op jit(solution)/shard_map/reduce_scatter | solution.py:39
  150.8 2.6 fusion.9
  153.4 0.0 all-gather.7.cloned.1.call-update
  153.4 0.0 all-gather.5.cloned.1.call-start
  153.5 0.5 all-gather.5.cloned.1.call-update
  154.0 0.0 reduce-scatter.11.cloned.1.call-start
  154.1 0.0 copy-done.7
  154.1 0.7 and_reduce_fusion
  154.8 39.8 %all-gather.7.cloned.1.call-done = bf16[1024,1376]{0,1:T(8,128)(2,1)} async-done(((bf16[256,1376]{0,1:T(8,128)(2,1)}), bf16[1024,1376]{0,1:T(8,128)(2,1)}) %all-gather.7.cloned.1.call-update) | async-done | bytes 2818064 | tf_op jit(solution)/shard_map/all_gather | solution.py:55
  194.6 6.1 %convolution_convert_fusion.3 = bf16[1024,1024]{1,0:T(8,128)(2,1)S(1)} fusion(bf16[1024,1376]{0,1:T(8,128)(2,1)} %all-gather.7.cloned.1.call-done, bf16[1376,1024]{1,0:T(8,128)(2,1)} %param.18), kind=kOutput, calls=%fused_computation.11 | convolution fusion | flops 2886729728 | bytes 7733248 | tf_op jit(solution)/shard_map/dot_general | solution.py:56
  200.7 0.2 slice.48
  200.9 0.1 broadcast_in_dim.13
  201.0 0.6 fusion.17
  201.6 1.9 pad_maximum_fusion
  203.5 0.0 reduce-scatter.11.cloned.1.call-update
  203.5 0.0 reduce-scatter.5.cloned.1.call-start
  203.5 26.3 %all-gather.5.cloned.1.call-done = bf16[320,4096]{1,0:T(8,128)(2,1)} async-done(((bf16[40,4096]{1,0:T(8,128)(2,1)}), bf16[320,4096]{1,0:T(8,128)(2,1)}) %all-gather.5.cloned.1.call-update) | async-done | bytes 2621456 | tf_op jit(solution)/shard_map/all_gather | solution.py:41
  229.8 1.8 conditional.1
  229.8 1.8 broadcast.40
  231.6 0.0 copy-start.4
  231.6 0.0 copy-start.1
  231.6 0.0 reduce-scatter.5.cloned.1.call-update
  231.6 37.3 %reduce-scatter.11.cloned.1.call-done = bf16[1,160,1024]{2,1,0:T(8,128)(2,1)} async-done(((bf16[8,160,1024]{2,1,0:T(8,128)(2,1)}), bf16[1,160,1024]{2,1,0:T(8,128)(2,1)}) %reduce-scatter.11.cloned.1.call-update) | async-done | bytes 327696 | tf_op jit(solution)/shard_map/reduce_scatter | solution.py:61
  268.9 3.7 %all-to-all-start.1 = ((bf16[4,40,1024]{2,1,0:T(8,128)(2,1)}), bf16[4,40,1024]{2,1,0:T(8,128)(2,1)S(1)}, u32[]{:S(2)}, u32[]{:S(2)}) async-start(bf16[4,40,1024]{2,1,0:T(8,128)(2,1)} %bitcast.41), calls=%async_computation.5 | async-start | bytes 655360 | tf_op jit(solution)/shard_map/all_to_all | solution.py:63
  272.7 5.5 %all-to-all-done.1 = bf16[4,40,1024]{2,1,0:T(8,128)(2,1)S(1)} async-done(((bf16[4,40,1024]{2,1,0:T(8,128)(2,1)}), bf16[4,40,1024]{2,1,0:T(8,128)(2,1)S(1)}, u32[]{:S(2)}, u32[]{:S(2)}) %all-to-all-start.1) | async-done | bytes 327712 | tf_op jit(solution)/shard_map/all_to_all | solution.py:63
  278.2 0.7 copy.38
  279.0 29.3 %reduce-scatter.5.cloned.1.call-done = bf16[40,4096]{1,0:T(8,128)(2,1)} async-done(((bf16[320,4096]{1,0:T(8,128)(2,1)}), bf16[40,4096]{1,0:T(8,128)(2,1)}) %reduce-scatter.5.cloned.1.call-update) | async-done | bytes 327696 | tf_op jit(solution)/shard_map/reduce_scatter | solution.py:52
  308.2 0.0 copy-done.4
  308.2 1.8 fusion.13
  310.0 0.0 copy-done.1
  (2 shorter events, 0.0 us)
Async XLA Ops:
  6.5 54.5 %copy-start = (bf16[1024,1376]{0,1:T(8,128)(2,1)S(1)}, bf16[1024,1376]{0,1:T(8,128)(2,1)}, u32[]{:S(2)}) copy-start(bf16[1024,1376]{0,1:T(8,128)(2,1)} %param.16) | copy-start | bytes 8454148
  6.5 48.8 %all-gather.9.cloned.1.call-start = ((), (), s32[]{:S(2)}) async-start(), calls=%async_computation.12 | async-start | bytes 2949120 | tf_op jit(solution)/shard_map/all_gather | solution.py:28
  9.0 49.7 %copy-start.3 = (bf16[40,4096]{1,0:T(8,128)(2,1)}, bf16[40,4096]{1,0:T(8,128)(2,1)S(1)}, u32[]{:S(2)}) copy-start(bf16[40,4096]{1,0:T(8,128)(2,1)S(1)} %fusion.12) | copy-start | bytes 983044
  21.9 84.6 %reduce-scatter.7.cloned.1.call-start = ((), (), s32[]{:S(2)}) async-start(), calls=%async_computation.8 | async-start | bytes 3522560 | tf_op jit(solution)/shard_map/reduce_scatter | solution.py:38
  55.3 3.6 %copy-start.2 = (bf16[4,320,1024]{2,0,1:T(4,128)(2,1)S(1)}, bf16[4,320,1024]{2,0,1:T(4,128)(2,1)}, u32[]{:S(2)}) copy-start(bf16[4,320,1024]{2,0,1:T(4,128)(2,1)} %all-gather.9.cloned.1.call-done) | copy-start | bytes 7864324
  59.7 1.3 copy-start.5
  66.0 1.5 copy-start.6
  66.0 84.7 %reduce-scatter.9.cloned.1.call-start = ((), (), s32[]{:S(2)}) async-start(), calls=%async_computation.9 | async-start | bytes 3522560 | tf_op jit(solution)/shard_map/reduce_scatter | solution.py:39
  74.4 79.6 %copy-start.7 = (s32[3]{0:T(128)S(1)}, s32[3]{0:T(128)}, u32[]{:S(2)}) copy-start(s32[3]{0:T(128)} %constant.55.clone.1) | copy-start | bytes 40
  74.4 120.1 %all-gather.7.cloned.1.call-start = ((), (), s32[]{:S(2)}) async-start(), calls=%async_computation.10 | async-start | bytes 3522560 | tf_op jit(solution)/shard_map/all_gather | solution.py:55
  153.4 76.4 %all-gather.5.cloned.1.call-start = ((), (), s32[]{:S(2)}) async-start(), calls=%async_computation.6 | async-start | bytes 2949120 | tf_op jit(solution)/shard_map/all_gather | solution.py:41
  154.0 114.9 %reduce-scatter.11.cloned.1.call-start = ((), (), s32[]{:S(2)}) async-start(), calls=%async_computation.11 | async-start | bytes 2949120 | tf_op jit(solution)/shard_map/reduce_scatter | solution.py:61
  203.5 104.7 %reduce-scatter.5.cloned.1.call-start = ((), (), s32[]{:S(2)}) async-start(), calls=%async_computation.7 | async-start | bytes 2949120 | tf_op jit(solution)/shard_map/reduce_scatter | solution.py:52
  231.6 76.6 %copy-start.4 = (bf16[40,4096]{1,0:T(8,128)(2,1)S(1)}, bf16[40,4096]{1,0:T(8,128)(2,1)}, u32[]{:S(2)}) copy-start(bf16[40,4096]{1,0:T(8,128)(2,1)} %param.13) | copy-start | bytes 983044
  231.6 78.4 %copy-start.1 = (bf16[1024,1376]{0,1:T(8,128)(2,1)S(1)}, bf16[1024,1376]{0,1:T(8,128)(2,1)}, u32[]{:S(2)}) copy-start(bf16[1024,1376]{0,1:T(8,128)(2,1)} %param.16) | copy-start | bytes 8454148
  268.9 9.3 %all-to-all-start.1 = ((bf16[4,40,1024]{2,1,0:T(8,128)(2,1)}), bf16[4,40,1024]{2,1,0:T(8,128)(2,1)S(1)}, u32[]{:S(2)}, u32[]{:S(2)}) async-start(bf16[4,40,1024]{2,1,0:T(8,128)(2,1)} %bitcast.41), calls=%async_computation.5 | async-start | bytes 655360 | tf_op jit(solution)/shard_map/all_to_all | solution.py:63
Sparse Core Ops, SparseCore 0:
  22.1 33.2 all-gather.8
  66.2 40.3 reduce-scatter.6
  109.6 41.1 reduce-scatter.8
  153.5 41.0 all-gather.6
  196.1 33.6 all-gather.4
  231.9 36.9 reduce-scatter.10
  271.2 36.9 reduce-scatter.4

commit v2 on v1

--- a/solution.py
+++ b/solution.py
@@ -1,11 +1,190 @@
 import jax
 import jax.numpy as jnp
 from jax import lax
+from jax.experimental import pallas as pl
+from jax.experimental.pallas import tpu as pltpu
 from jax.sharding import PartitionSpec as P
 
 norm_epsilon = 1e-05
 bf16 = jnp.bfloat16
 f32 = jnp.float32
+
+MESH = pl.DeviceIdType.MESH
+chunk_count = 2
+
+
+def plane_kernel(
+    n,
+    x_hbm,
+    gate_hbm,
+    up_hbm,
+    down_hbm,
+    out_ref,
+    x,
+    gate,
+    up,
+    down,
+    part,
+    own,
+    landed,
+    hidden,
+    load_sem,
+    part_send,
+    part_recv,
+    hid_send,
+    hid_recv,
+):
+    me = lax.axis_index("grp")
+    rows = part.shape[3]
+    loads = [
+        pltpu.make_async_copy(src, dst, load_sem.at[i])
+        for i, (src, dst) in enumerate(
+            ((x_hbm, x), (gate_hbm, gate), (up_hbm, up), (down_hbm, down))
+        )
+    ]
+    for load in loads:
+        load.start()
+    barrier = pltpu.get_barrier_semaphore()
+    for k in range(1, n):
+        pl.semaphore_signal(
+            barrier, inc=1, device_id={"grp": lax.rem(me + k, n)}, device_id_type=MESH
+        )
+    pl.semaphore_wait(barrier, n - 1)
+
+    def part_copy(d, src_slot, dst_slot, c):
+        return pltpu.make_async_remote_copy(
+            src_ref=part.at[src_slot, c],
+            dst_ref=landed.at[dst_slot, c],
+            send_sem=part_send.at[src_slot, c],
+            recv_sem=part_recv.at[dst_slot, c],
+            device_id={"grp": d},
+            device_id_type=MESH,
+        )
+
+    def hid_copy(d, owner, c):
+        return pltpu.make_async_remote_copy(
+            src_ref=hidden.at[owner, c],
+            dst_ref=hidden.at[owner, c],
+            send_sem=hid_send.at[d, c],
+            recv_sem=hid_recv.at[owner, c],
+            device_id={"grp": d},
+            device_id_type=MESH,
+        )
+
+    def peer(k):
+        return lax.rem(me + k, n)
+
+    loads[0].wait()
+    loads[1].wait()
+    loads[2].wait()
+
+    def send_step(s, carry):
+        c = s // (n - 1)
+        d = peer(n - 1 - s % (n - 1))
+        block = x[d, c]
+        part[d, c, 0] = jnp.dot(block, gate[...], preferred_element_type=f32).astype(bf16)
+        part[d, c, 1] = jnp.dot(block, up[...], preferred_element_type=f32).astype(bf16)
+        part_copy(d, d, me, c).start()
+        return carry
+
+    lax.fori_loop(0, chunk_count * (n - 1), send_step, 0)
+
+    def own_step(c, carry):
+        block = x[me, c]
+        own[c, 0] = jnp.dot(block, gate[...], preferred_element_type=f32)
+        own[c, 1] = jnp.dot(block, up[...], preferred_element_type=f32)
+        return carry
+
+    lax.fori_loop(0, chunk_count, own_step, 0)
+    loads[3].wait()
+
+    def hidden_step(c, carry):
+        for k in range(1, n):
+            part_copy(peer(k), peer(k), peer(k), c).wait_recv()
+
+        def tile(r, inner):
+            at = pl.ds(pl.multiple_of(r * 16, 16), 16)
+            g = own[c, 0, at, :]
+            u = own[c, 1, at, :]
+            for k in range(1, n):
+                g = g + landed[peer(k), c, 0, at, :].astype(f32)
+                u = u + landed[peer(k), c, 1, at, :].astype(f32)
+            hidden[me, c, at, :] = (g / (1.0 + jnp.exp(-g)) * u).astype(bf16)
+            return inner
+
+        lax.fori_loop(0, rows // 16, tile, 0)
+        for k in range(n - 1, 0, -1):
+            hid_copy(peer(k), me, c).start()
+        return carry
+
+    lax.fori_loop(0, chunk_count, hidden_step, 0)
+
+    def down_step(owner, c):
+        out_ref[owner, c] = jnp.dot(
+            hidden[owner, c], down[...], preferred_element_type=f32
+        ).astype(bf16)
+
+    def own_down(c, carry):
+        down_step(me, c)
+        return carry
+
+    lax.fori_loop(0, chunk_count, own_down, 0)
+
+    def peer_down(s, carry):
+        c = s // (n - 1)
+        d = peer(1 + s % (n - 1))
+        hid_copy(d, d, c).wait_recv()
+        down_step(d, c)
+        return carry
+
+    lax.fori_loop(0, chunk_count * (n - 1), peer_down, 0)
+
+    def drain(s, carry):
+        c = s // (n - 1)
+        d = peer(1 + s % (n - 1))
+        part_copy(d, d, me, c).wait_send()
+        hid_copy(d, me, c).wait_send()
+        return carry
+
+    lax.fori_loop(0, chunk_count * (n - 1), drain, 0)
+
+
+def plane_terms(x, gate, up, down, n):
+    rows, kslice = x.shape
+    units = gate.shape[1]
+    width = down.shape[1]
+    ch = rows // (n * chunk_count)
+    sems = pltpu.SemaphoreType.DMA
+    call = pl.pallas_call(
+        lambda *refs: plane_kernel(n, *refs),
+        out_shape=jax.ShapeDtypeStruct((n, chunk_count, ch, width), bf16),
+        in_specs=[pl.BlockSpec(memory_space=pl.ANY)] * 4,
+        out_specs=pl.BlockSpec(memory_space=pltpu.VMEM),
+        scratch_shapes=[
+            pltpu.VMEM((n, chunk_count, ch, kslice), bf16),
+            pltpu.VMEM((kslice, units), bf16),
+            pltpu.VMEM((kslice, units), bf16),
+            pltpu.VMEM((units, width), bf16),
+            pltpu.VMEM((n, chunk_count, 2, ch, units), bf16),
+            pltpu.VMEM((chunk_count, 2, ch, units), f32),
+            pltpu.VMEM((n, chunk_count, 2, ch, units), bf16),
+            pltpu.VMEM((n, chunk_count, ch, units), bf16),
+            sems((4,)),
+            sems((n, chunk_count)),
+            sems((n, chunk_count)),
+            sems((n, chunk_count)),
+            sems((n, chunk_count)),
+        ],
+        compiler_params=pltpu.CompilerParams(
+            collective_id=0, has_side_effects=True, vmem_limit_bytes=48 * 1024 * 1024
+        ),
+        cost_estimate=pl.CostEstimate(
+            flops=80_000_000_000, bytes_accessed=100_000_000, transcendentals=0
+        ),
+        name="plane",
+    )
+    out = call(x.reshape(n, chunk_count, ch, kslice), gate, up, down)
+    return out.reshape(rows, width)
 
 
 def on_device(
@@ -18,7 +197,6 @@
     n_spill = spill_blocks.shape[0]
     in_text = group == n_grp - 1
     kslice = image_gate.shape[0]
-    units = image_gate.shape[1]
     wide = tokens.astype(f32)
     scale = lax.rsqrt(jnp.mean(wide * wide, axis=-1, keepdims=True) + norm_epsilon)
     normed = (wide * scale * norm_gain).astype(bf16)
@@ -30,13 +208,10 @@
     spill_part = cols[n_grp - 1][spill_blocks].reshape(-1, kslice)
     x = jnp.concatenate([image_part, spill_part], axis=0)
     n_rows = x.shape[0]
-    step = 16 * n_grp
+    step = 16 * n_grp * chunk_count
     padded = (n_rows + step - 1) // step * step
     x = jnp.pad(x, ((0, padded - n_rows), (0, 0)))
-    part_gate = jnp.dot(x, image_gate, preferred_element_type=f32).astype(bf16)
-    part_up = jnp.dot(x, image_up, preferred_element_type=f32).astype(bf16)
-    gate = lax.psum_scatter(part_gate, "grp", scatter_dimension=0, tiled=True)
-    up = lax.psum_scatter(part_up, "grp", scatter_dimension=0, tiled=True)
+    terms = plane_terms(x, image_gate, image_up, image_down, n_grp)
 
     piece = lax.all_gather(normed, "tp", axis=0, tiled=True)
 
@@ -51,9 +226,6 @@
     )
     text_out = lax.psum_scatter(text_terms, "tp", scatter_dimension=0, tiled=True)
 
-    hidden = (jax.nn.silu(gate.astype(f32)) * up.astype(f32)).astype(bf16)
-    hidden = lax.all_gather(hidden, "grp", axis=0, tiled=True)
-    terms = jnp.dot(hidden, image_down, preferred_element_type=f32).astype(bf16)
     image_terms = terms[: (n_grp - 1) * n_tp * rows].reshape(n_grp - 1, n_tp, rows, kslice)
     spill_terms = terms[(n_grp - 1) * n_tp * rows : n_rows].reshape(n_spill, rows, kslice)
     placed = jnp.zeros((n_tp, rows, kslice), bf16).at[spill_blocks].set(spill_terms)

time: 317 us -> 246 us (0.78)
  waiting for transfers between devices: 248 us -> 93.7 us
  Pallas kernels: 0 us -> 101 us
  matrix products: 18 us -> 0 us
  local copies, waits for them, and re-layouts: 11.2 us -> 15.2 us
  other arithmetic: 10.1 us -> 6.61 us
    pallas_call x0 -> x1, Pallas kernels: none -> 101 us  [plane_terms(): out = call(x.reshape(n, chunk_count, ch, kslice), gate, up, down)]
    reduce_scatter x2 -> x0, waiting for transfers between devices: 76.3 us -> none  [the longest x1 44.3 us: on_device(): up = lax.psum_scatter(part_up, 'grp', scatter_dimension=0, tiled=True)]
    all_gather x1 -> x0, waiting for transfers between devices: 39.8 us -> none  [on_device(): hidden = lax.all_gather(hidden, 'grp', axis=0, tiled=True)]
    all_gather x1, waiting for transfers between devices: 26.3 us -> 0.02 us  [on_device(): piece = lax.all_gather(normed, 'tp', axis=0, tiled=True)]
    dot_general x3 -> x0, matrix products: 18 us -> none  [the longest x1 6.86 us: on_device(): part_up = jnp.dot(x, image_up, preferred_element_type=f32).astype(bf16)]
    all_gather x1, waiting for transfers between devices: 32.7 us -> 23.7 us  [on_device(): cols = lax.all_gather(cols, 'tp', axis=1, tiled=False)]
    unnamed x18 -> x16, local copies, waits for them, and re-layouts: 3.73 us -> 9.96 us
    reduce_scatter x1, waiting for transfers between devices: 37.3 us -> 33.6 us  [on_device(): lax.psum_scatter(every.reshape(n_tp, -1, kslice), 'tp', scatter_dimension...]
  transfers between devices with their start and end apart: 8 -> 5, of which waited for: 8 -> 4; matrix products, arithmetic and copies ran while one was open for 6% -> 6% of each run, Pallas kernels for 0% -> 41%
where the time goes in v2:
time: 246 us
  Pallas kernels  101 us (41%)
  waiting for transfers between devices  93.7 us (38%)
  local copies, waits for them, and re-layouts  15.2 us (6%)
  between operations  13.9 us (6%)
  blocking collectives  11.6 us (5%)
  other arithmetic  6.61 us (3%)
  starting transfers between devices  3.73 us (2%)
    pallas_call x1, Pallas kernels, plane_terms(): out = call(x.reshape(n, chunk_count, ch, kslice), gate, up, down)  101 us
    reduce_scatter x1, waiting for transfers between devices, on_device(): lax.psum_scatter(every.reshape(n_tp, -1, kslice), 'tp', scatter_dimension...  33.6 us
    reduce_scatter x1, waiting for transfers between devices, on_device(): lax.psum_scatter(text_terms, 'tp', scatter_dimension=0, tiled=True)  30.1 us
    all_gather x1, waiting for transfers between devices, on_device(): cols = lax.all_gather(cols, 'tp', axis=1, tiled=False)  23.7 us
    all_to_all x1, blocking collectives, on_device(): cols = lax.all_to_all(cols, 'grp', 0, 0, tiled=True)  11.6 us
    unnamed x16, local copies, waits for them, and re-layouts  9.96 us
    all_to_all x1, waiting for transfers between devices, on_device(): back = lax.all_to_all(mine, 'grp', 0, 0, tiled=True)  5.55 us
  transfers between devices with their start and end apart: 5, of which 4 were waited for; matrix products, arithmetic and copies ran while one was open for 6% of the time, Pallas kernels for 41%

profile of v2, /device:TPU:0, one launch (start us, length us, event | category | flops | bytes accessed | tf_op | source)
XLA Modules:
  0.0 246.1 jit_solution(13086622939982463248)
XLA Ops:
  6.5 0.0 copy-start.4
  6.5 0.0 all-gather.6.cloned.1.call-start
  6.5 1.3 fusion.5
  7.8 1.1 fusion.7
  9.0 0.0 copy-start.2
  9.0 0.2 reshape.77
  9.2 0.1 copy.38
  9.3 11.6 %all_to_all.10 = bf16[4,40,1024]{2,1,0:T(8,128)(2,1)S(1)} all-to-all(bf16[4,40,1024]{2,1,0:T(8,128)(2,1)S(1)} %copy.38), channel_id=1, replica_groups=mesh['grp'=4,'tp'=8] {'grp'}, dimensions={0} | all-to-all | bytes 655360 | tf_op jit(solution)/shard_map/all_to_all | solution.py:205
  20.9 1.0 copy.39
  21.9 0.0 all-gather.6.cloned.1.call-update
  21.9 0.0 all-gather.4.cloned.1.call-start
  22.0 0.0 copy-done.2
  22.0 0.7 all-gather.4.cloned.1.call-update
  22.7 0.0 reduce-scatter.5.cloned.1.call-start
  23.4 0.0 copy-done.4
  23.4 2.9 %copy.42.refs_1_ = bf16[1024,1376]{1,0:T(8,128)(2,1)} copy(bf16[1024,1376]{0,1:T(8,128)(2,1)S(1)} %copy-done.4) | data formatting | bytes 5636096 | tf_op args[3]
  26.3 0.0 copy-start.5
  26.3 4.6 %copy.43.refs_2_ = bf16[1024,1376]{1,0:T(8,128)(2,1)} copy(bf16[1024,1376]{0,1:T(8,128)(2,1)} %param.17) | data formatting | bytes 5636096 | tf_op args[4]
  30.9 0.0 copy-done.5
  30.9 0.7 and_reduce_fusion
  31.6 23.7 %all-gather.6.cloned.1.call-done = bf16[4,320,1024]{2,0,1:T(4,128)(2,1)} async-done(((bf16[4,40,1024]{2,0,1:T(4,128)(2,1)}), bf16[4,320,1024]{2,0,1:T(4,128)(2,1)}) %all-gather.6.cloned.1.call-update) | async-done | bytes 2621456 | tf_op jit(solution)/shard_map/all_gather | solution.py:206
  55.3 0.0 copy-start.1
  55.3 3.4 %slice.47 = bf16[1,320,1024]{2,0,1:T(2,128)(2,1)S(1)} slice(bf16[4,320,1024]{2,0,1:T(4,128)(2,1)} %all-gather.6.cloned.1.call-done), slice={[3:4], [0:320], [0:1024]} | slice | bytes 1310720 | tf_op jit(solution)/shard_map/slice | solution.py:208
  58.7 0.2 copy.49
  58.9 0.0 copy-done.1
  58.9 0.7 copy.48
  59.7 0.2 fusion.4
  59.9 101.1 %plane.1 = bf16[4,2,128,1024]{3,2,1,0:T(8,128)(2,1)S(1)} custom-call(bf16[4,2,128,1024]{3,2,1,0:T(8,128)(2,1)S(1)} %bitcast.28, bf16[1024,1376]{1,0:T(8,128)(2,1)} %copy.42.refs_1_, bf16[1024,1376]{1,0:T(8,128)(2,1)} %copy.43.refs_2_, bf16[1376,1024]{1,0:T(8,128)(2,1)} %refs_3_.1), custom_call_target="tpu_custom_call" | custom-call | flops 80000000000 | bytes 100000000 | tf_op jit(solution)/shard_map/plane/pallas_call | solution.py:186
  161.0 0.2 slice.48
  161.2 0.1 broadcast_in_dim.13
  161.3 0.6 fusion.10
  161.9 1.8 pad_maximum_fusion
  163.7 0.0 reduce-scatter.5.cloned.1.call-update
  163.7 0.0 reduce-scatter.3.cloned.1.call-start
  163.8 0.0 all-gather.4.cloned.1.call-done
  163.8 0.5 conditional.1
  163.8 0.3 broadcast.38
  164.3 0.0 copy-start
  164.3 0.0 copy-start.3
  164.3 1.5 copy-done
  165.8 0.0 reduce-scatter.3.cloned.1.call-update
  165.8 33.6 %reduce-scatter.5.cloned.1.call-done = bf16[1,160,1024]{2,1,0:T(8,128)(2,1)} async-done(((bf16[8,160,1024]{2,1,0:T(8,128)(2,1)}), bf16[1,160,1024]{2,1,0:T(8,128)(2,1)}) %reduce-scatter.5.cloned.1.call-update) | async-done | bytes 327696 | tf_op jit(solution)/shard_map/reduce_scatter | solution.py:233
  199.5 3.6 %all-to-all-start.1 = ((bf16[4,40,1024]{2,1,0:T(8,128)(2,1)}), bf16[4,40,1024]{2,1,0:T(8,128)(2,1)S(1)}, u32[]{:S(2)}, u32[]{:S(2)}) async-start(bf16[4,40,1024]{2,1,0:T(8,128)(2,1)} %bitcast.39), calls=%async_computation.3 | async-start | bytes 655360 | tf_op jit(solution)/shard_map/all_to_all | solution.py:235
  203.1 5.5 %all-to-all-done.1 = bf16[4,40,1024]{2,1,0:T(8,128)(2,1)S(1)} async-done(((bf16[4,40,1024]{2,1,0:T(8,128)(2,1)}), bf16[4,40,1024]{2,1,0:T(8,128)(2,1)S(1)}, u32[]{:S(2)}, u32[]{:S(2)}) %all-to-all-start.1) | async-done | bytes 327712 | tf_op jit(solution)/shard_map/all_to_all | solution.py:235
  208.7 30.1 %reduce-scatter.3.cloned.1.call-done = bf16[40,4096]{1,0:T(8,128)(2,1)} async-done(((bf16[320,4096]{1,0:T(8,128)(2,1)}), bf16[40,4096]{1,0:T(8,128)(2,1)}) %reduce-scatter.3.cloned.1.call-update) | async-done | bytes 327696 | tf_op jit(solution)/shard_map/reduce_scatter | solution.py:227
  238.7 0.0 copy-done.3
  238.7 0.8 fusion.8
  (3 shorter events, 0.0 us)
Async XLA Ops:
  6.5 16.8 %copy-start.4 = (bf16[1024,1376]{0,1:T(8,128)(2,1)S(1)}, bf16[1024,1376]{0,1:T(8,128)(2,1)}, u32[]{:S(2)}) copy-start(bf16[1024,1376]{0,1:T(8,128)(2,1)} %param.16) | copy-start | bytes 8454148
  6.5 48.8 %all-gather.6.cloned.1.call-start = ((), (), s32[]{:S(2)}) async-start(), calls=%async_computation.7 | async-start | bytes 2949120 | tf_op jit(solution)/shard_map/all_gather | solution.py:206
  9.0 13.0 %copy-start.2 = (bf16[40,4096]{1,0:T(8,128)(2,1)}, bf16[40,4096]{1,0:T(8,128)(2,1)S(1)}, u32[]{:S(2)}) copy-start(bf16[40,4096]{1,0:T(8,128)(2,1)S(1)} %fusion.7) | copy-start | bytes 983044
  21.9 141.9 %all-gather.4.cloned.1.call-start = ((), (), s32[]{:S(2)}) async-start(), calls=%async_computation.4 | async-start | bytes 2949120 | tf_op jit(solution)/shard_map/all_gather | solution.py:216
  22.7 176.8 %reduce-scatter.5.cloned.1.call-start = ((), (), s32[]{:S(2)}) async-start(), calls=%async_computation.6 | async-start | bytes 2949120 | tf_op jit(solution)/shard_map/reduce_scatter | solution.py:233
  26.3 4.6 %copy-start.5 = (s32[3]{0:T(128)S(1)}, s32[3]{0:T(128)}, u32[]{:S(2)}) copy-start(s32[3]{0:T(128)} %constant.52.clone.1) | copy-start | bytes 40
  55.3 3.6 %copy-start.1 = (bf16[4,320,1024]{2,0,1:T(4,128)(2,1)S(1)}, bf16[4,320,1024]{2,0,1:T(4,128)(2,1)}, u32[]{:S(2)}) copy-start(bf16[4,320,1024]{2,0,1:T(4,128)(2,1)} %all-gather.6.cloned.1.call-done) | copy-start | bytes 7864324
  163.7 75.0 %reduce-scatter.3.cloned.1.call-start = ((), (), s32[]{:S(2)}) async-start(), calls=%async_computation.5 | async-start | bytes 2949120 | tf_op jit(solution)/shard_map/reduce_scatter | solution.py:227
  164.3 1.5 copy-start
  164.3 74.4 %copy-start.3 = (bf16[40,4096]{1,0:T(8,128)(2,1)S(1)}, bf16[40,4096]{1,0:T(8,128)(2,1)}, u32[]{:S(2)}) copy-start(bf16[40,4096]{1,0:T(8,128)(2,1)} %param.13) | copy-start | bytes 983044
  199.5 9.2 %all-to-all-start.1 = ((bf16[4,40,1024]{2,1,0:T(8,128)(2,1)}), bf16[4,40,1024]{2,1,0:T(8,128)(2,1)S(1)}, u32[]{:S(2)}, u32[]{:S(2)}) async-start(bf16[4,40,1024]{2,1,0:T(8,128)(2,1)} %bitcast.39), calls=%async_computation.3 | async-start | bytes 655360 | tf_op jit(solution)/shard_map/all_to_all | solution.py:235
Sparse Core Ops, SparseCore 0:
  22.1 33.2 all-gather.5
  57.0 32.7 all-gather.3
  163.8 35.6 reduce-scatter.4
  201.6 37.0 reduce-scatter.2
